TPU v7x, 16 devices: a whole 2x2x2 slice. The times are simulated.
16 devices in a mesh: dp: 2 (over z), tp: 8 (over y, x, core).
Axes of the slice: x: 2, y: 2, z: 2, core: 2. Of those that a mesh axis runs over, the one named last changes fastest.
Arguments:
- hidden: bfloat16 [320, 512], P('dp'), parts along dimension 0
- positions: int32 [320], P('dp'), parts along dimension 0
- self_keys: bfloat16 [2, 320, 448, 8, 64], P(None, 'dp', None, 'tp'), parts along dimension 1
- self_vals: bfloat16 [2, 320, 448, 8, 64], P(None, 'dp', None, 'tp'), parts along dimension 1
- cross_keys: bfloat16 [2, 64, 1500, 8, 64], P(None, 'dp', None, 'tp'), parts along dimension 1
- cross_vals: bfloat16 [2, 64, 1500, 8, 64], P(None, 'dp', None, 'tp'), parts along dimension 1
- ln_gain: bfloat16 [2, 3, 512], replicated
- ln_bias: bfloat16 [2, 3, 512], replicated
- w_query: bfloat16 [2, 512, 512], P(None, None, 'tp')
- b_query: bfloat16 [2, 512], P(None, 'tp')
- w_key: bfloat16 [2, 512, 512], P(None, None, 'tp')
- w_value: bfloat16 [2, 512, 512], P(None, None, 'tp')
- b_value: bfloat16 [2, 512], P(None, 'tp')
- w_out: bfloat16 [2, 512, 512], P(None, 'tp')
- b_out: bfloat16 [2, 512], replicated
- w_cquery: bfloat16 [2, 512, 512], P(None, None, 'tp')
- b_cquery: bfloat16 [2, 512], P(None, 'tp')
- w_cout: bfloat16 [2, 512, 512], P(None, 'tp')
- b_cout: bfloat16 [2, 512], replicated
- w_fc1: bfloat16 [2, 512, 2048], P(None, None, 'tp')
- b_fc1: bfloat16 [2, 2048], P(None, 'tp')
- w_fc2: bfloat16 [2, 2048, 512], P(None, 'tp')
- b_fc2: bfloat16 [2, 512], replicated
Outputs:
- output 1: bfloat16 [320, 512], P('dp'), parts along dimension 0
- output 2: bfloat16 [2, 320, 448, 8, 64], P(None, 'dp', None, 'tp'), parts along dimension 1
- output 3: bfloat16 [2, 320, 448, 8, 64], P(None, 'dp', None, 'tp'), parts along dimension 1
There are 2 independent parts. A program takes and returns all parts, laid end to end along the dimension named above; an argument that names none is the same for every part.
All inputs are finite; a program needn't handle non-finite values.
Results may differ from a plain program's by a relative error of at most 0.02.
Values are sent between devices in bfloat16 or wider.
A program may use at most 1 GiB of HBM per device.

v0:
```python
import jax
import jax.numpy as jnp
from jax import lax
from jax.sharding import PartitionSpec as P

EPS = 1e-5
PARAM_NAMES = ('ln_gain', 'ln_bias', 'w_query', 'b_query', 'w_key', 'w_value', 'b_value', 'w_out', 'b_out', 'w_cquery', 'b_cquery', 'w_cout', 'b_cout', 'w_fc1', 'b_fc1', 'w_fc2', 'b_fc2')


def layer_norm(values, gain_row, bias_row):
    wide_vals = values.astype(jnp.float32)
    center = wide_vals - jnp.mean(wide_vals, axis=-1, keepdims=True)
    var_est = jnp.mean(center * center, axis=-1, keepdims=True)
    return (center * lax.rsqrt(var_est + EPS) * gain_row + bias_row).astype(jnp.bfloat16)


def tp_sum(part_out):
    return lax.psum(part_out.astype(jnp.bfloat16), 'tp')


def decoder_layer(hidden, positions, cache_k, cache_v, cross_k, cross_v, layer_w, group_sum):
    batch_size = hidden.shape[0]
    head_count = cache_k.shape[2]
    head_dim = cache_k.shape[3]
    audios = cross_k.shape[0]
    beam_count = batch_size // audios
    qk_scale = head_dim ** -0.25
    slot_ids = lax.broadcasted_iota(jnp.int32, (1, cache_k.shape[1]), 1)
    slot_hit = (slot_ids == positions[:, None])[:, :, None, None]
    slot_mask = (slot_ids <= positions[:, None])[:, None, :]

    normed = layer_norm(hidden, layer_w['ln_gain'][0], layer_w['ln_bias'][0])
    query_heads = ((jnp.dot(normed, layer_w['w_query'], preferred_element_type=jnp.float32) + layer_w['b_query']) * qk_scale).astype(jnp.bfloat16).reshape(batch_size, head_count, head_dim)
    new_key = (jnp.dot(normed, layer_w['w_key'], preferred_element_type=jnp.float32) * qk_scale).astype(jnp.bfloat16).reshape(batch_size, 1, head_count, head_dim)
    new_val = (jnp.dot(normed, layer_w['w_value'], preferred_element_type=jnp.float32) + layer_w['b_value']).astype(jnp.bfloat16).reshape(batch_size, 1, head_count, head_dim)
    cache_k = jnp.where(slot_hit, new_key, cache_k)
    cache_v = jnp.where(slot_hit, new_val, cache_v)
    raw_scores = jnp.einsum('bhd,bshd->bhs', query_heads, cache_k, preferred_element_type=jnp.float32)
    attn_probs = jax.nn.softmax(jnp.where(slot_mask, raw_scores, -1e30), axis=-1).astype(jnp.bfloat16)
    attn_out = jnp.einsum('bhs,bshd->bhd', attn_probs, cache_v, preferred_element_type=jnp.float32).astype(jnp.bfloat16).reshape(batch_size, head_count * head_dim)
    attn_sum = group_sum(jnp.dot(attn_out, layer_w['w_out'], preferred_element_type=jnp.float32))
    hidden = (hidden.astype(jnp.float32) + attn_sum + layer_w['b_out']).astype(jnp.bfloat16)

    normed = layer_norm(hidden, layer_w['ln_gain'][1], layer_w['ln_bias'][1])
    cross_query = ((jnp.dot(normed, layer_w['w_cquery'], preferred_element_type=jnp.float32) + layer_w['b_cquery']) * qk_scale).astype(jnp.bfloat16).reshape(audios, beam_count, head_count, head_dim)
    cross_scores = jnp.einsum('abhd,afhd->abhf', cross_query, cross_k, preferred_element_type=jnp.float32)
    cross_probs = jax.nn.softmax(cross_scores, axis=-1).astype(jnp.bfloat16)
    cross_out = jnp.einsum('abhf,afhd->abhd', cross_probs, cross_v, preferred_element_type=jnp.float32).astype(jnp.bfloat16).reshape(batch_size, head_count * head_dim)
    cross_sum = group_sum(jnp.dot(cross_out, layer_w['w_cout'], preferred_element_type=jnp.float32))
    hidden = (hidden.astype(jnp.float32) + cross_sum + layer_w['b_cout']).astype(jnp.bfloat16)

    normed = layer_norm(hidden, layer_w['ln_gain'][2], layer_w['ln_bias'][2])
    mlp_inner = jax.nn.gelu(jnp.dot(normed, layer_w['w_fc1'], preferred_element_type=jnp.float32) + layer_w['b_fc1'], approximate=False).astype(jnp.bfloat16)
    mlp_sum = group_sum(jnp.dot(mlp_inner, layer_w['w_fc2'], preferred_element_type=jnp.float32))
    hidden = (hidden.astype(jnp.float32) + mlp_sum + layer_w['b_fc2']).astype(jnp.bfloat16)
    return hidden, cache_k, cache_v


def solution(mesh):
    cache_spec = P(None, 'dp', None, 'tp', None)
    col_spec = P(None, None, 'tp')
    row_spec = P(None, 'tp', None)
    vec_spec = P(None, 'tp')
    param_specs = {'ln_gain': P(), 'ln_bias': P(), 'w_query': col_spec, 'b_query': vec_spec, 'w_key': col_spec, 'w_value': col_spec, 'b_value': vec_spec, 'w_out': row_spec, 'b_out': P(), 'w_cquery': col_spec, 'b_cquery': vec_spec, 'w_cout': row_spec, 'b_cout': P(), 'w_fc1': col_spec, 'b_fc1': vec_spec, 'w_fc2': row_spec, 'b_fc2': P()}
    in_specs = (P('dp', None), P('dp'), cache_spec, cache_spec, cache_spec, cache_spec) + tuple(param_specs[param_name] for param_name in PARAM_NAMES)

    def local_step(hidden, positions, self_keys, self_vals, cross_keys, cross_vals, *layer_params):
        keys_out = []
        vals_out = []
        for layer_idx in range(self_keys.shape[0]):
            layer_w = {param_name: stacked[layer_idx] for param_name, stacked in zip(PARAM_NAMES, layer_params)}
            hidden, cache_k, cache_v = decoder_layer(hidden, positions, self_keys[layer_idx], self_vals[layer_idx], cross_keys[layer_idx], cross_vals[layer_idx], layer_w, tp_sum)
            keys_out.append(cache_k)
            vals_out.append(cache_v)
        return hidden, jnp.stack(keys_out), jnp.stack(vals_out)

    return jax.shard_map(local_step, mesh=mesh, in_specs=in_specs, out_specs=(P('dp', None), cache_spec, cache_spec), check_vma=False)
```

profile of v0, /device:TPU:0, one launch (start us, length us, event | category | flops | bytes accessed | tf_op | source)
XLA Modules:
  0.0 385.0 jit_solution(2439950185107819723)
XLA Ops:
  7.2 1.0 convert_reduce_fusion.5
  8.3 1.1 fusion.78
  9.4 0.7 bitcast_convert_fusion.2
  10.1 0.7 bitcast_convert_fusion.1
  10.9 0.8 slice_convert_fusion.2
  11.6 0.8 slice_convert_fusion.1
  12.4 0.8 iota_compare_fusion
  13.2 1.1 fusion.81
  14.3 1.0 fusion.33
  15.4 1.0 fusion.32
  16.6 1.0 fusion.40
  17.7 5.1 %fusion.3 = f32[160,1,448]{2,1,0:T(1,128)S(1)} fusion(bf16[160,64,1]{1,2,0:T(2,128)(2,1)S(1)} %copy.66, pred[160,448]{1,0:T(8,128)(4,1)S(1)} %iota_compare_fusion, bf16[2,160,448,1,64]{2,4,1,3,0:T(8,128)(2,1)} %bitcast.225, bf16[160,64]{1,0:T(8,128)(2,1)S(1)} %copy.46), kind=kOutput, calls=%fused_computation.10 | convolution fusion | flops 13762560 | bytes 10885120 | tf_op jit(solution)/shard_map/bhd,bshd->bhs/dot_general | solution.py:38
  23.0 0.2 fusion.96
  23.5 4.3 %copy-done = bf16[2,160,448,1,64]{2,4,3,1,0:T(8,128)(2,1)S(1)} copy-done((bf16[2,160,448,1,64]{2,4,3,1,0:T(8,128)(2,1)S(1)}, bf16[2,160,448,1,64]{2,4,3,1,0:T(8,128)(2,1)}, u32[]{:S(2)}) %copy-start) | copy-done | bytes 18350104
  27.8 3.7 fusion.2
  31.4 0.9 convolution_convert_fusion.5
  32.4 48.8 %all-reduce.7.cloned.1.call-done = bf16[160,512]{1,0:T(8,128)(2,1)} async-done(((bf16[160,512]{1,0:T(8,128)(2,1)}), bf16[160,512]{1,0:T(8,128)(2,1)}) %all-reduce.7.cloned.1.call-update) | async-done | bytes 163856 | tf_op jit(solution)/shard_map/psum | solution.py:18
  81.3 1.1 convert_reduce_fusion.4
  82.6 0.3 fusion.38
  83.0 3.9 %fusion.319 = (f32[32,5]{1,0:T(8,128)S(1)}, f32[32,5,1,1500]{3,1,0,2:T(8,128)S(1)}) fusion(bf16[32,5,64]{2,1,0:T(8,128)(2,1)S(1)} %reshape.358, bf16[2,32,1500,1,64]{2,4,1,3,0:T(8,128)(2,1)} %bitcast.232), kind=kOutput, calls=%fused_computation.410 | convolution fusion | flops 30959840 | bytes 7272576 | tf_op jit(solution)/shard_map/abhd,afhd->abhf/dot_general | solution.py:46
  86.9 0.4 fusion.22
  87.3 4.6 %fusion.27 = bf16[32,5,1,64]{3,1,0,2:T(8,128)(2,1)S(1)} fusion(bf16[2,32,1500,1,64]{2,4,1,3,0:T(8,128)(2,1)} %bitcast.256, f32[32,5,1,1500]{3,1,0,2:T(8,128)S(1)} %get-tuple-element.49, f32[32,5]{1,0:T(8,128)S(1)} %fusion.22, f32[32,5]{1,0:T(8,128)S(1)} %get-tuple-element.48), kind=kOutput, calls=%fused_computation.53 | convolution fusion | flops 31450240 | bytes 7273216 | tf_op jit(solution)/shard_map/abhf,afhd->abhd/dot_general | solution.py:48
  92.0 0.8 convolution_convert_fusion.4
  93.0 45.5 %all-reduce.9.cloned.1.call-done = bf16[160,512]{1,0:T(8,128)(2,1)} async-done(((bf16[160,512]{1,0:T(8,128)(2,1)}), bf16[160,512]{1,0:T(8,128)(2,1)}) %all-reduce.9.cloned.1.call-update) | async-done | bytes 163856 | tf_op jit(solution)/shard_map/psum | solution.py:18
  138.4 1.1 convert_reduce_fusion.3
  139.7 1.5 convolution_convert_fusion.1
  141.3 46.3 %all-reduce.11.cloned.1.call-done = bf16[160,512]{1,0:T(8,128)(2,1)} async-done(((bf16[160,512]{1,0:T(8,128)(2,1)}), bf16[160,512]{1,0:T(8,128)(2,1)}) %all-reduce.11.cloned.1.call-update) | async-done | bytes 163856 | tf_op jit(solution)/shard_map/psum | solution.py:18
  187.5 1.1 convert_reduce_fusion.2
  189.9 24.7 %broadcast_select_fusion.1 = (bf16[1,160,448,1,64]{2,4,1,3,0:T(8,128)(2,1)}, bf16[1,160,448,1,64]{2,4,1,3,0:T(8,128)(2,1)}, bf16[1,160,448,1,64]{2,4,3,1,0:T(8,128)(2,1)}) fusion(pred[160,448]{1,0:T(8,128)(4,1)S(1)} %iota_compare_fusion, bf16[2,160,448,1,64]{2,4,1,3,0:T(8,128)(2,1)} %bitcast.226, bf16[160,64]{1,0:T(8,128)(2,1)S(1)} %copy.46, ...), kind=kLoop, calls=%fused_computation.13 | loop fusion | flops 13762560 | bytes 55183360 | tf_op jit(solution)/shard_map/jit(_where)/select_n | solution.py:36
  214.7 5.1 %fusion.1 = f32[160,1,448]{2,1,0:T(1,128)S(1)} fusion(bf16[160,64,1]{1,2,0:T(2,128)(2,1)S(1)} %copy.70, pred[160,448]{1,0:T(8,128)(4,1)S(1)} %iota_compare_fusion, bf16[2,160,448,1,64]{2,4,1,3,0:T(8,128)(2,1)} %bitcast.227, bf16[160,64]{1,0:T(8,128)(2,1)S(1)} %copy.53), kind=kOutput, calls=%fused_computation.6 | convolution fusion | flops 13762560 | bytes 10885120 | tf_op jit(solution)/shard_map/bhd,bshd->bhs/dot_general | solution.py:38
  220.0 0.2 fusion.97
  220.4 3.7 fusion
  224.1 0.8 convolution_convert_fusion.3
  225.2 10.3 %bitcast_select_fusion = bf16[1,160,448,1,64]{2,4,3,1,0:T(8,128)(2,1)} fusion(pred[160,448]{1,0:T(8,128)(4,1)S(1)} %iota_compare_fusion, bf16[2,160,448,1,64]{2,4,3,1,0:T(8,128)(2,1)} %param.26, bf16[160,64]{1,0:T(8,128)(2,1)S(1)} %copy.55), kind=kLoop, calls=%fused_computation.2 | loop fusion | flops 4587520 | bytes 18442240 | tf_op jit(solution)/shard_map/jit(_where)/select_n | solution.py:37
  235.5 35.1 %all-reduce.13.cloned.1.call-done = bf16[160,512]{1,0:T(8,128)(2,1)} async-done(((bf16[160,512]{1,0:T(8,128)(2,1)}), bf16[160,512]{1,0:T(8,128)(2,1)}) %all-reduce.13.cloned.1.call-update) | async-done | bytes 163856 | tf_op jit(solution)/shard_map/psum | solution.py:18
  270.6 1.1 convert_reduce_fusion.1
  271.8 0.3 fusion.36
  272.3 3.8 fusion.320
  276.1 0.4 fusion.23
  276.5 4.6 %fusion.26 = bf16[32,5,1,64]{3,1,0,2:T(8,128)(2,1)S(1)} fusion(bf16[2,32,1500,1,64]{2,4,1,3,0:T(8,128)(2,1)} %bitcast.257, f32[32,5,1,1500]{3,1,0,2:T(8,128)S(1)} %get-tuple-element.51, f32[32,5]{1,0:T(8,128)S(1)} %fusion.23, f32[32,5]{1,0:T(8,128)S(1)} %get-tuple-element.50), kind=kOutput, calls=%fused_computation.52 | convolution fusion | flops 31450240 | bytes 7273216 | tf_op jit(solution)/shard_map/abhf,afhd->abhd/dot_general | solution.py:48
  281.1 0.8 convolution_convert_fusion.2
  282.0 17.4 %maximum_bitcast_fusion = bf16[2,160,448,1,64]{2,4,3,1,0:T(8,128)(2,1)} fusion(bf16[1,160,448,1,64]{2,4,1,3,0:T(8,128)(2,1)} %get-tuple-element.20, bf16[1,160,448,1,64]{2,4,1,3,0:T(8,128)(2,1)} %get-tuple-element.19), kind=kLoop, calls=%fused_computation | loop fusion | flops 9175040 | bytes 36700160
  299.4 28.2 %all-reduce.15.cloned.1.call-done = bf16[160,512]{1,0:T(8,128)(2,1)} async-done(((bf16[160,512]{1,0:T(8,128)(2,1)}), bf16[160,512]{1,0:T(8,128)(2,1)}) %all-reduce.15.cloned.1.call-update) | async-done | bytes 163856 | tf_op jit(solution)/shard_map/psum | solution.py:18
  327.5 1.1 convert_reduce_fusion
  328.8 1.5 convolution_convert_fusion
  330.3 17.4 %pad_maximum_fusion = bf16[2,160,448,1,64]{2,4,3,1,0:T(8,128)(2,1)} fusion(bf16[1,160,448,1,64]{2,4,3,1,0:T(8,128)(2,1)} %bitcast_select_fusion, bf16[1,160,448,1,64]{2,4,3,1,0:T(8,128)(2,1)} %get-tuple-element.21), kind=kLoop, calls=%fused_computation.1 | loop fusion | flops 9175040 | bytes 36700160 | tf_op jit(solution)/shard_map/stack | solution.py:75
  347.6 28.8 %all-reduce.17.cloned.1.call-done = bf16[160,512]{1,0:T(8,128)(2,1)} async-done(((bf16[160,512]{1,0:T(8,128)(2,1)}), bf16[160,512]{1,0:T(8,128)(2,1)}) %all-reduce.17.cloned.1.call-update) | async-done | bytes 163856 | tf_op jit(solution)/shard_map/psum | solution.py:18
  376.5 1.6 fusion.93
  (96 shorter events, 4.2 us)
Async XLA Ops:
  7.2 74.1 %all-reduce.7.cloned.1.call-start = ((), (), s32[]{:S(2)}) async-start(), calls=%async_computation | async-start | bytes 327680 | tf_op jit(solution)/shard_map/psum | solution.py:18
  17.7 5.1 %copy-start.5 = (s32[160]{0:T(256)S(1)}, s32[160]{0:T(256)}, u32[]{:S(2)}) copy-start(s32[160]{0:T(256)} %param.24) | copy-start | bytes 1924
  17.7 10.0 %copy-start = (bf16[2,160,448,1,64]{2,4,3,1,0:T(8,128)(2,1)S(1)}, bf16[2,160,448,1,64]{2,4,3,1,0:T(8,128)(2,1)}, u32[]{:S(2)}) copy-start(bf16[2,160,448,1,64]{2,4,3,1,0:T(8,128)(2,1)} %param.26) | copy-start | bytes 55050244
  27.7 3.7 copy-start.2
  27.7 4.6 %copy-start.6 = (bf16[2,512]{1,0:T(2,128)(2,1)S(1)}, bf16[2,512]{1,0:T(2,128)(2,1)}, u32[]{:S(2)}) copy-start(bf16[2,512]{1,0:T(2,128)(2,1)} %param.37) | copy-start | bytes 6148
  27.7 4.7 %copy-start.7 = (bf16[2,512]{1,0:T(2,128)(2,1)S(1)}, bf16[2,512]{1,0:T(2,128)(2,1)}, u32[]{:S(2)}) copy-start(bf16[2,512]{1,0:T(2,128)(2,1)} %param.41) | copy-start | bytes 6148
  27.7 4.7 %copy-start.10 = (bf16[2,64]{1,0:T(2,128)(2,1)S(1)}, bf16[2,64]{1,0:T(2,128)(2,1)}, u32[]{:S(2)}) copy-start(bf16[2,64]{1,0:T(2,128)(2,1)} %param.39) | copy-start | bytes 772
  27.7 53.5 %copy-start.1 = (bf16[160,512]{1,0:T(8,128)(2,1)S(1)}, bf16[160,512]{1,0:T(8,128)(2,1)}, u32[]{:S(2)}) copy-start(bf16[160,512]{1,0:T(8,128)(2,1)} %param.23) | copy-start | bytes 491524
  27.8 54.8 %copy-start.15 = (bf16[2,512,64]{1,2,0:T(8,128)(2,1)S(1)}, bf16[2,512,64]{1,2,0:T(8,128)(2,1)}, u32[]{:S(2)}) copy-start(bf16[2,512,64]{1,2,0:T(8,128)(2,1)} %param.38) | copy-start | bytes 393220
  32.3 106.1 %all-reduce.9.cloned.1.call-start = ((), (), s32[]{:S(2)}) async-start(), calls=%async_computation.1 | async-start | bytes 327680 | tf_op jit(solution)/shard_map/psum | solution.py:18
  83.0 9.0 %copy-start.4 = (bf16[2,64,512]{2,1,0:T(8,128)(2,1)S(1)}, bf16[2,64,512]{2,1,0:T(8,128)(2,1)}, u32[]{:S(2)}) copy-start(bf16[2,64,512]{2,1,0:T(8,128)(2,1)} %param.40) | copy-start | bytes 393220
  83.0 9.9 %copy-start.9 = (bf16[2,256]{1,0:T(2,128)(2,1)S(1)}, bf16[2,256]{1,0:T(2,128)(2,1)}, u32[]{:S(2)}) copy-start(bf16[2,256]{1,0:T(2,128)(2,1)} %param.43) | copy-start | bytes 3076
  83.0 56.7 %copy-start.11 = (bf16[2,256,512]{2,1,0:T(8,128)(2,1)S(1)}, bf16[2,256,512]{2,1,0:T(8,128)(2,1)}, u32[]{:S(2)}) copy-start(bf16[2,256,512]{2,1,0:T(8,128)(2,1)} %param.44) | copy-start | bytes 1572868
  83.0 56.7 %copy-start.12 = (bf16[2,512,256]{2,1,0:T(8,128)(2,1)S(1)}, bf16[2,512,256]{2,1,0:T(8,128)(2,1)}, u32[]{:S(2)}) copy-start(bf16[2,512,256]{2,1,0:T(8,128)(2,1)} %param.42) | copy-start | bytes 1572868
  86.9 54.3 %copy-start.8 = (bf16[2,512]{1,0:T(2,128)(2,1)S(1)}, bf16[2,512]{1,0:T(2,128)(2,1)}, u32[]{:S(2)}) copy-start(bf16[2,512]{1,0:T(2,128)(2,1)} %param.45) | copy-start | bytes 6148
  86.9 102.0 %copy-start.3 = (bf16[2,512,64]{1,2,0:T(8,128)(2,1)S(1)}, bf16[2,512,64]{1,2,0:T(8,128)(2,1)}, u32[]{:S(2)}) copy-start(bf16[2,512,64]{1,2,0:T(8,128)(2,1)} %param.33) | copy-start | bytes 393220
  87.3 101.8 %copy-start.13 = (bf16[2,512,64]{1,2,0:T(8,128)(2,1)S(1)}, bf16[2,512,64]{1,2,0:T(8,128)(2,1)}, u32[]{:S(2)}) copy-start(bf16[2,512,64]{1,2,0:T(8,128)(2,1)} %param.34) | copy-start | bytes 393220
  87.3 102.1 %copy-start.14 = (bf16[2,512,64]{1,2,0:T(8,128)(2,1)S(1)}, bf16[2,512,64]{1,2,0:T(8,128)(2,1)}, u32[]{:S(2)}) copy-start(bf16[2,512,64]{1,2,0:T(8,128)(2,1)} %param.31) | copy-start | bytes 393220
  92.9 94.7 %all-reduce.11.cloned.1.call-start = ((), (), s32[]{:S(2)}) async-start(), calls=%async_computation.2 | async-start | bytes 327680 | tf_op jit(solution)/shard_map/psum | solution.py:18
  141.2 129.3 %all-reduce.13.cloned.1.call-start = ((), (), s32[]{:S(2)}) async-start(), calls=%async_computation.3 | async-start | bytes 327680 | tf_op jit(solution)/shard_map/psum | solution.py:18
  189.9 30.5 %slice-start = ((s8[20971520]{0:T(1024)(128)(4,1)}), s8[4194304]{0:T(1024)(128)(4,1)S(1)}, s32[]{:S(2)}) async-start(s8[20971520]{0:T(1024)(128)(4,1)} %bitcast.230), calls=%async_computation.6 | async-start | bytes 8388608
  189.9 30.5 %slice-start.1 = ((s8[20971520]{0:T(1024)(128)(4,1)}), s8[4194304]{0:T(1024)(128)(4,1)S(1)}, s32[]{:S(2)}) async-start(s8[20971520]{0:T(1024)(128)(4,1)} %bitcast.230), calls=%async_computation.7 | async-start | bytes 8388608
  189.9 30.5 %slice-start.2 = ((s8[20971520]{0:T(1024)(128)(4,1)}), s8[4194304]{0:T(1024)(128)(4,1)S(1)}, s32[]{:S(2)}) async-start(s8[20971520]{0:T(1024)(128)(4,1)} %bitcast.230), calls=%async_computation.8 | async-start | bytes 8388608
  189.9 30.5 %slice-start.3 = ((s8[20971520]{0:T(1024)(128)(4,1)}), s8[4194304]{0:T(1024)(128)(4,1)S(1)}, s32[]{:S(2)}) async-start(s8[20971520]{0:T(1024)(128)(4,1)} %bitcast.230), calls=%async_computation.9 | async-start | bytes 8388608
  214.7 5.8 %slice-start.4 = ((s8[20971520]{0:T(1024)(128)(4,1)}), s8[4194304]{0:T(1024)(128)(4,1)S(1)}, s32[]{:S(2)}) async-start(s8[20971520]{0:T(1024)(128)(4,1)} %bitcast.230), calls=%async_computation.10 | async-start | bytes 8388608
  225.0 102.5 %all-reduce.15.cloned.1.call-start = ((), (), s32[]{:S(2)}) async-start(), calls=%async_computation.4 | async-start | bytes 327680 | tf_op jit(solution)/shard_map/psum | solution.py:18
  282.0 94.5 %all-reduce.17.cloned.1.call-start = ((), (), s32[]{:S(2)}) async-start(), calls=%async_computation.5 | async-start | bytes 327680 | tf_op jit(solution)/shard_map/psum | solution.py:18
Sparse Core Ops, SparseCore 0:
  32.4 48.7 all-reduce.6
  93.0 45.3 all-reduce.8
  142.1 45.3 all-reduce.10
  225.1 45.3 all-reduce.12
  282.1 45.3 all-reduce.14
  331.1 45.3 all-reduce.16
where the time goes:
time: 386 us; the launch traced here: 385 us
  waiting for transfers between devices  233 us (60%)
  other arithmetic  86.9 us (23%)
  matrix products  44.8 us (12%)
  between operations  14.6 us (4%)
  local copies, waits for them, and re-layouts  5.44 us (1%)
    psum x6, waiting for transfers between devices, tp_sum(): return lax.psum(part_out.astype(jnp.bfloat16), 'tp')  233 us
    select_n x1, other arithmetic, decoder_layer(): cache_k = jnp.where(slot_hit, new_key, cache_k)  24.7 us
    unnamed x2, other arithmetic  17.4 us
    another operation x1, other arithmetic, local_step(): return (hidden, jnp.stack(keys_out), jnp.stack(vals_out))  17.4 us
    select_n x1, other arithmetic, decoder_layer(): cache_v = jnp.where(slot_hit, new_val, cache_v)  10.3 us
    dot_general x2, matrix products, decoder_layer(): jnp.einsum('bhd,bshd->bhs', query_heads, cache_k, preferred_element_type=...  10.2 us
    dot_general x2, matrix products, decoder_layer(): jnp.einsum('abhf,afhd->abhd', cross_probs, cross_v, preferred_element_typ...  9.19 us
  transfers between devices with their start and end apart: 6, of which 6 were waited for; matrix products, arithmetic and copies ran while one was open for 12% of the time, Pallas kernels for 0%

commit v1 on v0

v1 whole, which is shorter than its diff:
```python
import functools

import jax
import jax.numpy as jnp
from jax import lax
from jax.experimental import pallas as pl
from jax.experimental.pallas import tpu as pltpu
from jax.sharding import PartitionSpec as P

EPS = 1e-5
F32 = jnp.float32
BF16 = jnp.bfloat16
NT = (((1,), (1,)), ((), ()))
MESH = pl.DeviceIdType.MESH
PARAM_NAMES = ('ln_gain', 'ln_bias', 'w_query', 'b_query', 'w_key', 'w_value', 'b_value', 'w_out', 'b_out', 'w_cquery', 'b_cquery', 'w_cout', 'b_cout', 'w_fc1', 'b_fc1', 'w_fc2', 'b_fc2')

BATCH = 160
AUD = 32
BEAMS = 5
HD = 64
CTX = 448
FRAMES = 1500
D = 512
TP = 8
SCALE = HD ** -0.25
GB = 8
GROUPS = BATCH // GB
GA = 8
AGROUPS = AUD // GA
GR = GA * BEAMS


def layer_norm(wide, gain, bias):
    center = wide - jnp.mean(wide, axis=-1, keepdims=True)
    var_est = jnp.mean(center * center, axis=-1, keepdims=True)
    return (center * lax.rsqrt(var_est + EPS) * gain + bias).astype(BF16)


def row_of(ref, *idx):
    return ref[idx].astype(F32)


def dot_nt(a, b):
    return lax.dot_general(a, b, NT, preferred_element_type=F32)


def dot(a, b):
    return jnp.dot(a, b, preferred_element_type=F32)


def fold_heads(wide, keep):
    wide = jnp.where(keep, wide, 0.0)
    part = (wide[:, 0:128] + wide[:, 128:256]) + (wide[:, 256:384] + wide[:, 384:512])
    return part[:, :HD] + part[:, HD:]


def self_kernel(layer, pos_ref, h_ref, gain_ref, bias_ref, wq_ref, bq_ref, wk_ref, wv_ref, bv_ref, kin, vin, *rest):
    if layer:
        rest = rest[2:]
    o_ref, kout, vout, kbuf, vbuf, q_scr, a_scr, kt_scr, vt_scr, o_scr, in_sem, out_sem = rest

    def rows(g):
        return pl.ds(pl.multiple_of(g * GB, GB), GB)

    def fetch(g, which):
        src, buf = ((kin, kbuf), (vin, vbuf))[which]
        return pltpu.make_async_copy(src.at[layer, rows(g)], buf.at[rows(g)], in_sem.at[which, g])

    def put(g, which):
        buf, dst = ((kbuf, kout), (vbuf, vout))[which]
        return pltpu.make_async_copy(buf.at[rows(g)], dst.at[layer, rows(g)], out_sem.at[which, g])

    def start_fetch(g, carry):
        fetch(g, 0).start()
        fetch(g, 1).start()
        return carry

    lax.fori_loop(0, GROUPS, start_fetch, 0)

    normed = layer_norm(h_ref[...].astype(F32), row_of(gain_ref, 0, pl.ds(layer, 1)), row_of(bias_ref, 0, pl.ds(layer, 1)))
    query = ((dot_nt(normed, wq_ref[layer]) + row_of(bq_ref, pl.ds(layer, 1))) * SCALE).astype(BF16).astype(F32)
    q_scr[...] = jnp.concatenate([query, query], axis=1)
    a_scr[...] = normed.astype(F32)
    eye = lax.broadcasted_iota(jnp.int32, (HD, HD), 0) == lax.broadcasted_iota(jnp.int32, (HD, HD), 1)
    bv_col = jnp.sum(jnp.where(eye, row_of(bv_ref, pl.ds(layer, 1)), 0.0), axis=1, keepdims=True)

    def project(g, carry):
        part = a_scr[rows(g)].astype(BF16)
        kt_scr[g] = dot_nt(wk_ref[layer], part) * SCALE
        vt_scr[g] = dot_nt(wv_ref[layer], part) + bv_col
        return carry

    lax.fori_loop(0, GROUPS, project, 0, unroll=4)

    lane128 = lax.broadcasted_iota(jnp.int32, (HD, 128), 1)
    lane64 = lax.broadcasted_iota(jnp.int32, (HD, HD), 1) + 384
    lane_ctx = lax.broadcasted_iota(jnp.int32, (GB, CTX), 1)
    row_id = lax.broadcasted_iota(jnp.int32, (GB, 1), 0)
    keep = lax.broadcasted_iota(jnp.int32, (GB, D), 1) // HD == lax.broadcasted_iota(jnp.int32, (GB, D), 0)

    def attend(g, carry):
        fetch(g, 0).wait()
        fetch(g, 1).wait()
        pos_col = jnp.zeros((GB, 1), jnp.int32)
        for j in range(GB):
            beam = g * GB + j
            pos = pos_ref[beam]
            pos_col = jnp.where(row_id == j, pos, pos_col)
            off = pl.multiple_of(jnp.minimum(pos // 128, 2) * 128, 128)
            for buf, col_scr in ((kbuf, kt_scr), (vbuf, vt_scr)):
                col = jnp.broadcast_to(col_scr[g][:, j:j + 1], (HD, 128)).astype(BF16)
                view = buf.at[beam, :, pl.ds(off, 128)]
                view[...] = jnp.where(lane128 + off == pos, col, view[...])
                tail = buf.at[beam, :, pl.ds(384, 64)]
                tail[...] = jnp.where(lane64 == pos, col[:, :HD], tail[...])
        q8 = q_scr[rows(g)]
        qblk = jnp.where(keep, jnp.concatenate([q8, q8, q8, q8], axis=1), 0.0).astype(BF16)
        score = dot(qblk, kbuf[rows(g)].reshape(GB * HD, CTX))
        score = jnp.where(lane_ctx <= pos_col, score, -1e30)
        expd = jnp.exp(score - jnp.max(score, axis=1, keepdims=True))
        probs = (expd / jnp.sum(expd, axis=1, keepdims=True)).astype(BF16)
        wide = dot_nt(probs, vbuf[rows(g)].reshape(GB * HD, CTX))
        o_scr[rows(g)] = fold_heads(wide, keep)
        put(g, 0).start()
        put(g, 1).start()
        return carry

    lax.fori_loop(0, GROUPS, attend, 0)
    o_ref[...] = jnp.concatenate([o_scr[0:80], o_scr[80:160]], axis=1).astype(BF16)

    def finish(g, carry):
        put(g, 0).wait()
        put(g, 1).wait()
        return carry

    lax.fori_loop(0, GROUPS, finish, 0)


def erf_gelu(x):
    return 0.5 * x * (1.0 + lax.erf(x * (2.0 ** -0.5)))


def mid_kernel(layer, h_ref, o_ref, gain_ref, bias_ref, wo_ref, bo_ref, wcq_ref, bcq_ref, wco_ref, bco_ref, w1_ref, b1_ref, w2_ref, b2_ref,
               kin, vin, out_ref, kbuf, vbuf, wofull, wcofull, obuf1, obuf2, o2_ref, q_scr, o_scr, pbuf, rbuf, base_scr, hblk, hfull,
               ck_sem, send_sem, recv_sem):
    me = lax.axis_index('tp')
    peers = [lax.rem(me + d, TP) for d in range(1, TP)]

    def auds(g):
        return pl.ds(pl.multiple_of(g * GA, GA), GA)

    def fetch(g, which):
        src, buf = ((kin, kbuf), (vin, vbuf))[which]
        return pltpu.make_async_copy(src.at[layer, auds(g)], buf.at[auds(g)], ck_sem.at[which, g])

    for g in range(AGROUPS):
        fetch(g, 0).start()
        fetch(g, 1).start()

    barrier = pltpu.get_barrier_semaphore()
    for peer in peers:
        pl.semaphore_signal(barrier, inc=1, device_id={'tp': peer}, device_id_type=MESH)
    pl.semaphore_wait(barrier, TP - 1)

    def send(phase, src, dst, peer):
        return pltpu.make_async_remote_copy(src_ref=src, dst_ref=dst, send_sem=send_sem.at[phase, peer], recv_sem=recv_sem.at[phase, me],
                                            device_id={'tp': peer}, device_id_type=MESH)

    def arrival(phase, dst, peer):
        return pltpu.make_async_remote_copy(src_ref=dst, dst_ref=dst, send_sem=send_sem.at[phase, peer], recv_sem=recv_sem.at[phase, peer],
                                            device_id={'tp': peer}, device_id_type=MESH)

    def gather_start(phase, src, slots):
        for peer in peers:
            send(phase, src, slots.at[me], peer).start()

    def gather_wait(phase, src, slots):
        for peer in peers:
            arrival(phase, slots.at[peer], peer).wait_recv()
        for peer in peers:
            send(phase, src, slots.at[me], peer).wait_send()

    gather_start(0, o_ref, obuf1)
    gather_start(1, wo_ref.at[layer], wofull)
    gather_start(2, wco_ref.at[layer], wcofull)
    obuf1[me] = o_ref[...]
    wofull[me] = wo_ref[layer]
    wcofull[me] = wco_ref[layer]

    low = lax.broadcasted_iota(jnp.int32, (80, 128), 1) < HD

    def head_rows(slots):
        top, bottom = [], []
        for pair in range(TP // 2):
            left = slots[2 * pair].astype(F32)
            right = slots[2 * pair + 1].astype(F32)
            top.append(jnp.where(low, left, pltpu.roll(right, HD, 1)))
            bottom.append(jnp.where(low, pltpu.roll(left, HD, 1), right))
        return jnp.concatenate([jnp.concatenate(top, axis=1), jnp.concatenate(bottom, axis=1)], axis=0).astype(BF16)

    gather_wait(0, o_ref, obuf1)
    gather_wait(1, wo_ref.at[layer], wofull)
    hid = h_ref[...].astype(F32) + (dot(head_rows(obuf1), wofull[...].reshape(D, D)) + row_of(bo_ref, pl.ds(layer, 1)))
    hid = hid.astype(BF16).astype(F32)
    normed = layer_norm(hid, row_of(gain_ref, 1, pl.ds(layer, 1)), row_of(bias_ref, 1, pl.ds(layer, 1)))
    query = ((dot_nt(normed, wcq_ref[layer]) + row_of(bcq_ref, pl.ds(layer, 1))) * SCALE).astype(BF16).astype(F32)
    q_scr[...] = jnp.concatenate([query, query], axis=1)

    keep = lax.broadcasted_iota(jnp.int32, (GR, D), 1) // HD == lax.broadcasted_iota(jnp.int32, (GR, D), 0) // BEAMS

    def attend(g, carry):
        fetch(g, 0).wait()
        fetch(g, 1).wait()
        rows = pl.ds(pl.multiple_of(g * GR, GR), GR)
        q40 = q_scr[rows]
        qblk = jnp.where(keep, jnp.concatenate([q40, q40, q40, q40], axis=1), 0.0).astype(BF16)
        score = dot(qblk, kbuf[auds(g)].reshape(GA * HD, FRAMES))
        expd = jnp.exp(score - jnp.max(score, axis=1, keepdims=True))
        probs = (expd / jnp.sum(expd, axis=1, keepdims=True)).astype(BF16)
        wide = dot_nt(probs, vbuf[auds(g)].reshape(GA * HD, FRAMES))
        o_scr[rows] = fold_heads(wide, keep)
        return carry

    lax.fori_loop(0, AGROUPS, attend, 0)
    o2_ref[...] = jnp.concatenate([o_scr[0:80], o_scr[80:160]], axis=1).astype(BF16)
    gather_start(3, o2_ref, obuf2)
    obuf2[me] = o2_ref[...]
    gather_wait(2, wco_ref.at[layer], wcofull)
    gather_wait(3, o2_ref, obuf2)
    hid = hid + (dot(head_rows(obuf2), wcofull[...].reshape(D, D)) + row_of(bco_ref, pl.ds(layer, 1)))
    hid = hid.astype(BF16).astype(F32)

    normed = layer_norm(hid, row_of(gain_ref, 2, pl.ds(layer, 1)), row_of(bias_ref, 2, pl.ds(layer, 1)))
    inner = erf_gelu(dot(normed, w1_ref[layer]) + row_of(b1_ref, pl.ds(layer, 1))).astype(BF16)
    part = dot(inner, w2_ref[layer]).astype(BF16)
    for t in range(TP):
        pbuf[t] = part[80 * (t % 2):80 * (t % 2) + 80, 128 * (t // 2):128 * (t // 2) + 128]
    base_scr[...] = hid + row_of(b2_ref, pl.ds(layer, 1))
    for peer in peers:
        send(4, pbuf.at[peer], rbuf.at[me], peer).start()
    rbuf[me] = pbuf[me]
    for peer in peers:
        arrival(4, rbuf.at[peer], peer).wait_recv()
    for peer in peers:
        send(4, pbuf.at[peer], rbuf.at[me], peer).wait_send()

    def block(t):
        return pl.ds(pl.multiple_of(80 * lax.rem(t, 2), 80), 80), pl.ds(pl.multiple_of(128 * lax.div(t, 2), 128), 128)

    mine = block(me)
    total = rbuf[0].astype(F32)
    for t in range(1, TP):
        total = total + rbuf[t].astype(F32)
    hblk[...] = (base_scr[mine] + total).astype(BF16)
    for peer in peers:
        send(5, hblk, hfull.at[mine], peer).start()
    hfull[mine] = hblk[...]
    for peer in peers:
        arrival(5, hfull.at[block(peer)], peer).wait_recv()
    for peer in peers:
        send(5, hblk, hfull.at[mine], peer).wait_send()
    out_ref[...] = hfull[...]


VM = pl.BlockSpec(memory_space=pltpu.VMEM)
ANY = pl.BlockSpec(memory_space=pltpu.HBM)
SM = pl.BlockSpec(memory_space=pltpu.SMEM)


def self_call(layer, positions, hidden, w, keys, vals, prev):
    cache = jax.ShapeDtypeStruct(keys.shape, BF16)
    args = [positions, hidden, w['ln_gain'], w['ln_bias'], w['w_query'], w['b_query'], w['w_key'], w['w_value'], w['b_value'], keys, vals] + list(prev)
    specs = [SM] + [VM] * 8 + [ANY] * (2 + len(prev))
    return pl.pallas_call(
        functools.partial(self_kernel, layer),
        out_shape=(jax.ShapeDtypeStruct((BATCH // 2, 2 * HD), BF16), cache, cache),
        in_specs=specs,
        out_specs=(VM, ANY, ANY),
        input_output_aliases={11: 1, 12: 2} if prev else {},
        scratch_shapes=[
            pltpu.VMEM((BATCH, HD, CTX), BF16),
            pltpu.VMEM((BATCH, HD, CTX), BF16),
            pltpu.VMEM((BATCH, 2 * HD), F32),
            pltpu.VMEM((BATCH, D), F32),
            pltpu.VMEM((GROUPS, HD, GB), F32),
            pltpu.VMEM((GROUPS, HD, GB), F32),
            pltpu.VMEM((BATCH, HD), F32),
            pltpu.SemaphoreType.DMA((2, GROUPS)),
            pltpu.SemaphoreType.DMA((2, GROUPS)),
        ],
        compiler_params=pltpu.CompilerParams(vmem_limit_bytes=40 * 2 ** 20),
        name=f'self_attention_{layer}',
    )(*args)


def mid_call(layer, hidden, heads, w, cross_k, cross_v):
    names = ('ln_gain', 'ln_bias', 'w_out', 'b_out', 'w_cquery', 'b_cquery', 'w_cout', 'b_cout', 'w_fc1', 'b_fc1', 'w_fc2', 'b_fc2')
    args = [hidden, heads] + [w[name] for name in names] + [cross_k, cross_v]
    return pl.pallas_call(
        functools.partial(mid_kernel, layer),
        out_shape=jax.ShapeDtypeStruct((BATCH, D), BF16),
        in_specs=[VM] * (2 + len(names)) + [ANY] * 2,
        out_specs=VM,
        scratch_shapes=[
            pltpu.VMEM((AUD, HD, FRAMES), BF16),
            pltpu.VMEM((AUD, HD, FRAMES), BF16),
            pltpu.VMEM((TP, HD, D), BF16),
            pltpu.VMEM((TP, HD, D), BF16),
            pltpu.VMEM((TP, BATCH // 2, 2 * HD), BF16),
            pltpu.VMEM((TP, BATCH // 2, 2 * HD), BF16),
            pltpu.VMEM((BATCH // 2, 2 * HD), BF16),
            pltpu.VMEM((BATCH, 2 * HD), F32),
            pltpu.VMEM((BATCH, HD), F32),
            pltpu.VMEM((TP, 80, 128), BF16),
            pltpu.VMEM((TP, 80, 128), BF16),
            pltpu.VMEM((BATCH, D), F32),
            pltpu.VMEM((80, 128), BF16),
            pltpu.VMEM((BATCH, D), BF16),
            pltpu.SemaphoreType.DMA((2, AGROUPS)),
            pltpu.SemaphoreType.DMA((6, TP)),
            pltpu.SemaphoreType.DMA((6, TP)),
        ],
        compiler_params=pltpu.CompilerParams(vmem_limit_bytes=40 * 2 ** 20, collective_id=layer, has_side_effects=True),
        name=f'cross_mlp_{layer}',
    )(*args)


def solution(mesh):
    cache_spec = P(None, 'dp', None, 'tp', None)
    col_spec = P(None, None, 'tp')
    row_spec = P(None, 'tp', None)
    vec_spec = P(None, 'tp')
    param_specs = {'ln_gain': P(), 'ln_bias': P(), 'w_query': col_spec, 'b_query': vec_spec, 'w_key': col_spec, 'w_value': col_spec, 'b_value': vec_spec, 'w_out': row_spec, 'b_out': P(), 'w_cquery': col_spec, 'b_cquery': vec_spec, 'w_cout': row_spec, 'b_cout': P(), 'w_fc1': col_spec, 'b_fc1': vec_spec, 'w_fc2': row_spec, 'b_fc2': P()}
    in_specs = (P('dp', None), P('dp'), cache_spec, cache_spec, cache_spec, cache_spec) + tuple(param_specs[param_name] for param_name in PARAM_NAMES)

    def lanes_last(cache):
        return jnp.transpose(cache, (0, 1, 3, 4, 2)).reshape(cache.shape[0], cache.shape[1], cache.shape[4], cache.shape[2])

    def slots_back(cache):
        layers, beams, width, slots = cache.shape
        return jnp.transpose(cache.reshape(layers, beams, 1, width, slots), (0, 1, 4, 2, 3))

    def local_step(hidden, positions, self_keys, self_vals, cross_keys, cross_vals, *layer_params):
        w = dict(zip(PARAM_NAMES, layer_params))
        for name in ('w_query', 'w_key', 'w_value', 'w_cquery'):
            w[name] = jnp.transpose(w[name], (0, 2, 1))
        for name in ('ln_gain', 'ln_bias'):
            w[name] = jnp.transpose(w[name], (1, 0, 2))
        keys, vals, cross_k, cross_v = (lanes_last(c) for c in (self_keys, self_vals, cross_keys, cross_vals))
        prev = ()
        for layer in range(2):
            heads, *prev = self_call(layer, positions, hidden, w, keys, vals, prev)
            hidden = mid_call(layer, hidden, heads, w, cross_k, cross_v)
        return hidden, slots_back(prev[0]), slots_back(prev[1])

    return jax.shard_map(local_step, mesh=mesh, in_specs=in_specs, out_specs=(P('dp', None), cache_spec, cache_spec), check_vma=False)
```

time: 386 us -> 118 us (0.31)
  waiting for transfers between devices: 233 us -> 0 us
  Pallas kernels: 0 us -> 104 us
  other arithmetic: 86.9 us -> 0 us
  matrix products: 44.8 us -> 0 us
  between operations: 14.6 us -> 0.94 us
  local copies, waits for them, and re-layouts: 5.44 us -> 12.3 us
    psum x6 -> x0, waiting for transfers between devices: 233 us -> none  [tp_sum(): return lax.psum(part_out.astype(jnp.bfloat16), 'tp')]
    pallas_call x0 -> x4, Pallas kernels: none -> 104 us  [the longest x2 65.5 us: mid_call(): pl.pallas_call(functools.partial(mid_kernel, layer), out_shape=jax.ShapeD...]
    dot_general x22 -> x0, matrix products: 44.8 us -> none  [the longest x2 10.2 us: decoder_layer(): jnp.einsum('bhd,bshd->bhs', query_heads, cache_k, preferred_element_type=...]
    select_n x2 -> x0, other arithmetic: 35 us -> none  [the longest x1 24.7 us: decoder_layer(): cache_k = jnp.where(slot_hit, new_key, cache_k)]
    unnamed x2 -> x0, other arithmetic: 17.4 us -> none
    another operation x1 -> x0, other arithmetic: 17.4 us -> none  [local_step(): return (hidden, jnp.stack(keys_out), jnp.stack(vals_out))]
    reduce_sum x16 -> x0, other arithmetic: 9.73 us -> none  [the longest x6 6.3 us: layer_norm(): center = wide_vals - jnp.mean(wide_vals, axis=-1, keepdims=True)]
    unnamed x42 -> x55, local copies, waits for them, and re-layouts: 4.38 us -> 12.3 us
  transfers between devices with their start and end apart: 6 -> 0, of which waited for: 6 -> 0; matrix products, arithmetic and copies ran while one was open for 12% -> 0% of each run, Pallas kernels for 0% -> 0%
where the time goes in v1:
time: 118 us
  Pallas kernels  104 us (88%)
  local copies, waits for them, and re-layouts  12.3 us (10%)
    pallas_call x2, Pallas kernels, mid_call(): pl.pallas_call(functools.partial(mid_kernel, layer), out_shape=jax.ShapeD...  65.5 us
    pallas_call x2, Pallas kernels, self_call(): pl.pallas_call(functools.partial(self_kernel, layer), out_shape=(jax.Shap...  39 us
    unnamed x55, local copies, waits for them, and re-layouts  12.3 us

profile of v1, /device:TPU:0, one launch (start us, length us, event | category | flops | bytes accessed | tf_op | source)
XLA Modules:
  0.0 117.7 jit_solution(7304712305436188697)
XLA Ops:
  0.6 0.0 copy-start.4
  0.6 0.9 copy-done.4
  1.6 0.0 copy-start.6
  1.6 0.9 copy-done.6
  2.5 0.9 copy-done.8
  3.4 0.9 copy-done.10
  4.3 0.7 copy-done.15
  5.0 0.7 copy-done.17
  5.7 0.7 copy-done.22
  6.3 0.7 copy-done.25
  7.0 0.7 copy-done.26
  7.7 0.0 copy-start.12
  7.7 0.0 copy-start.13
  7.7 0.0 copy-start.14
  7.7 0.0 copy-start.16
  7.7 0.0 copy-start.18
  7.7 0.0 copy-start.19
  7.7 0.0 copy-start.20
  7.7 0.0 copy-start.21
  7.7 0.0 copy-start.23
  7.7 0.0 copy-start.24
  7.8 19.5 %self_attention_0.1 = (bf16[80,128]{1,0:T(8,128)(2,1)S(1)}, bf16[2,160,64,448]{3,2,1,0:T(8,128)(2,1)}, bf16[2,160,64,448]{3,2,1,0:T(8,128)(2,1)}) custom-call(s32[160]{0:T(256)S(1)} %copy-done.22, bf16[160,512]{1,0:T(8,128)(2,1)S(1)} %copy-done.4, bf16[3,2,512]{2,1,0:T(2,128)(2,1)S(1)} %bitcast.46, bf16[3,2,512]{2,1,0:T(2,128)(2,1)S(1)} %bitcast.50, ...), custom_call_target="tpu_custom_call" | custom-call | tf_op jit(solution)/shard_map/self_attention_0/pallas_call | solution.py:274
  27.2 0.0 copy-start.7
  27.2 0.0 copy-start.9
  27.3 0.0 copy-start.11
  27.3 0.0 copy-done
  27.3 0.0 copy-done.2
  27.3 0.0 copy-done.3
  27.3 0.0 copy-done.5
  27.3 0.0 copy-done.12
  27.3 0.0 copy-done.13
  27.3 0.0 copy-done.14
  27.3 0.0 copy-done.16
  27.3 0.0 copy-done.18
  27.4 0.0 copy-done.19
  27.4 0.0 copy-done.20
  27.4 0.0 copy-done.21
  27.4 0.0 copy-done.23
  27.4 0.0 copy-done.24
  27.4 33.8 %cross_mlp_0.1.h_ref = bf16[160,512]{1,0:T(8,128)(2,1)S(1)} custom-call(bf16[160,512]{1,0:T(8,128)(2,1)S(1)} %copy-done.5, bf16[80,128]{1,0:T(8,128)(2,1)S(1)} %get-tuple-element.9.o_ref, bf16[3,2,512]{2,1,0:T(2,128)(2,1)S(1)} %bitcast.47, bf16[3,2,512]{2,1,0:T(2,128)(2,1)S(1)} %bitcast.51, bf16[2,64,512]{2,1,0:T(8,128)(2,1)S(1)} %copy-done.12, ...), custom_call_target="tpu_custom_call" | custom-call | tf_op jit(solution)/shard_map/cross_mlp_0/pallas_call | solution.py:299
  61.2 0.0 copy-done.7
  61.2 0.0 copy-done.9
  61.3 0.0 copy-done.11
  61.3 19.5 %self_attention_1.1 = (bf16[80,128]{1,0:T(8,128)(2,1)S(1)}, bf16[2,160,64,448]{3,2,1,0:T(8,128)(2,1)}, bf16[2,160,64,448]{3,2,1,0:T(8,128)(2,1)}) custom-call(s32[160]{0:T(256)S(1)} %copy-done.22, bf16[160,512]{1,0:T(8,128)(2,1)S(1)} %cross_mlp_0.1.h_ref, bf16[3,2,512]{2,1,0:T(2,128)(2,1)S(1)} %bitcast.48, ...), custom_call_target="tpu_custom_call", output_to_operand_aliasing={{1}: (11, {}), {2}: (12, {})} | custom-call | tf_op jit(solution)/shard_map/self_attention_1/pallas_call | solution.py:274
  80.8 0.0 copy-start.1
  80.8 4.6 %copy-done.1 = bf16[2,32,1500,1,64]{2,4,3,1,0:T(8,128)(2,1)S(1)} copy-done((bf16[2,32,1500,1,64]{2,4,3,1,0:T(8,128)(2,1)S(1)}, bf16[2,32,1500,1,64]{2,4,3,1,0:T(8,128)(2,1)}, u32[]{:S(2)}) %copy-start.1) | copy-done | bytes 12288024
  85.4 31.7 %cross_mlp_1.1 = bf16[160,512]{1,0:T(8,128)(2,1)S(1)} custom-call(bf16[160,512]{1,0:T(8,128)(2,1)S(1)} %cross_mlp_0.1.h_ref, bf16[80,128]{1,0:T(8,128)(2,1)S(1)} %get-tuple-element.12.o_ref, bf16[3,2,512]{2,1,0:T(2,128)(2,1)S(1)} %bitcast.49, bf16[3,2,512]{2,1,0:T(2,128)(2,1)S(1)} %bitcast.53, bf16[2,64,512]{2,1,0:T(8,128)(2,1)S(1)} %copy-done.12, ...), custom_call_target="tpu_custom_call" | custom-call | tf_op jit(solution)/shard_map/cross_mlp_1/pallas_call | solution.py:299
  117.0 0.7 copy.37
  (11 shorter events, 0.0 us)
Async XLA Ops:
  0.6 0.9 copy-start.4
  1.6 0.9 copy-start.6
  2.5 0.9 copy-start.8
  3.4 0.9 copy-start.10
  4.3 0.7 copy-start.15
  5.0 0.7 copy-start.17
  5.7 0.7 copy-start.22
  6.3 0.7 copy-start.25
  7.0 0.7 copy-start.26
  7.6 19.6 %copy-start = (bf16[2,32,1500,1,64]{2,4,3,1,0:T(8,128)(2,1)S(1)}, bf16[2,32,1500,1,64]{2,4,3,1,0:T(8,128)(2,1)}, u32[]{:S(2)}) copy-start(bf16[2,32,1500,1,64]{2,4,3,1,0:T(8,128)(2,1)} %param.27) | copy-start | bytes 36864004
  7.6 19.6 %copy-start.2 = (bf16[2,512,256]{2,1,0:T(8,128)(2,1)S(1)}, bf16[2,512,256]{2,1,0:T(8,128)(2,1)}, u32[]{:S(2)}) copy-start(bf16[2,512,256]{2,1,0:T(8,128)(2,1)} %w1_ref.3) | copy-start | bytes 1572868
  7.6 19.6 %copy-start.3 = (bf16[2,256,512]{2,1,0:T(8,128)(2,1)S(1)}, bf16[2,256,512]{2,1,0:T(8,128)(2,1)}, u32[]{:S(2)}) copy-start(bf16[2,256,512]{2,1,0:T(8,128)(2,1)} %w2_ref.3) | copy-start | bytes 1572868
  7.7 19.7 %copy-start.5 = (bf16[160,512]{1,0:T(8,128)(2,1)S(1)}, bf16[160,512]{1,0:T(8,128)(2,1)}, u32[]{:S(2)}) copy-start(bf16[160,512]{1,0:T(8,128)(2,1)} %h_ref.3) | copy-start | bytes 491524
  7.7 19.7 %copy-start.12 = (bf16[2,64,512]{2,1,0:T(8,128)(2,1)S(1)}, bf16[2,64,512]{2,1,0:T(8,128)(2,1)}, u32[]{:S(2)}) copy-start(bf16[2,64,512]{2,1,0:T(8,128)(2,1)} %wo_ref.3) | copy-start | bytes 393220
  7.7 19.7 %copy-start.13 = (bf16[2,512,64]{1,2,0:T(8,128)(2,1)S(1)}, bf16[2,512,64]{1,2,0:T(8,128)(2,1)}, u32[]{:S(2)}) copy-start(bf16[2,512,64]{1,2,0:T(8,128)(2,1)} %param.38) | copy-start | bytes 393220
  7.7 19.7 %copy-start.14 = (bf16[2,64,512]{2,1,0:T(8,128)(2,1)S(1)}, bf16[2,64,512]{2,1,0:T(8,128)(2,1)}, u32[]{:S(2)}) copy-start(bf16[2,64,512]{2,1,0:T(8,128)(2,1)} %wco_ref.3) | copy-start | bytes 393220
  7.7 19.7 %copy-start.16 = (bf16[2,3,512]{2,0,1:T(2,128)(2,1)S(1)}, bf16[2,3,512]{2,0,1:T(2,128)(2,1)}, u32[]{:S(2)}) copy-start(bf16[2,3,512]{2,0,1:T(2,128)(2,1)} %param.29) | copy-start | bytes 18436
  7.7 19.7 %copy-start.18 = (bf16[2,3,512]{2,0,1:T(2,128)(2,1)S(1)}, bf16[2,3,512]{2,0,1:T(2,128)(2,1)}, u32[]{:S(2)}) copy-start(bf16[2,3,512]{2,0,1:T(2,128)(2,1)} %param.30) | copy-start | bytes 18436
  7.7 19.7 %copy-start.19 = (bf16[2,512]{1,0:T(2,128)(2,1)S(1)}, bf16[2,512]{1,0:T(2,128)(2,1)}, u32[]{:S(2)}) copy-start(bf16[2,512]{1,0:T(2,128)(2,1)} %bo_ref.3) | copy-start | bytes 6148
  7.7 19.7 %copy-start.20 = (bf16[2,512]{1,0:T(2,128)(2,1)S(1)}, bf16[2,512]{1,0:T(2,128)(2,1)}, u32[]{:S(2)}) copy-start(bf16[2,512]{1,0:T(2,128)(2,1)} %bco_ref.3) | copy-start | bytes 6148
  7.7 19.7 %copy-start.21 = (bf16[2,512]{1,0:T(2,128)(2,1)S(1)}, bf16[2,512]{1,0:T(2,128)(2,1)}, u32[]{:S(2)}) copy-start(bf16[2,512]{1,0:T(2,128)(2,1)} %b2_ref.3) | copy-start | bytes 6148
  7.7 19.7 %copy-start.23 = (bf16[2,256]{1,0:T(2,128)(2,1)S(1)}, bf16[2,256]{1,0:T(2,128)(2,1)}, u32[]{:S(2)}) copy-start(bf16[2,256]{1,0:T(2,128)(2,1)} %b1_ref.3) | copy-start | bytes 3076
  7.7 19.7 %copy-start.24 = (bf16[2,64]{1,0:T(2,128)(2,1)S(1)}, bf16[2,64]{1,0:T(2,128)(2,1)}, u32[]{:S(2)}) copy-start(bf16[2,64]{1,0:T(2,128)(2,1)} %bcq_ref.3) | copy-start | bytes 772
  27.2 34.0 %copy-start.7 = (bf16[2,512,64]{1,2,0:T(8,128)(2,1)S(1)}, bf16[2,512,64]{1,2,0:T(8,128)(2,1)}, u32[]{:S(2)}) copy-start(bf16[2,512,64]{1,2,0:T(8,128)(2,1)} %param.31) | copy-start | bytes 393220
  27.2 34.0 %copy-start.9 = (bf16[2,512,64]{1,2,0:T(8,128)(2,1)S(1)}, bf16[2,512,64]{1,2,0:T(8,128)(2,1)}, u32[]{:S(2)}) copy-start(bf16[2,512,64]{1,2,0:T(8,128)(2,1)} %param.33) | copy-start | bytes 393220
  27.3 34.0 %copy-start.11 = (bf16[2,512,64]{1,2,0:T(8,128)(2,1)S(1)}, bf16[2,512,64]{1,2,0:T(8,128)(2,1)}, u32[]{:S(2)}) copy-start(bf16[2,512,64]{1,2,0:T(8,128)(2,1)} %param.34) | copy-start | bytes 393220
  80.8 4.6 %copy-start.1 = (bf16[2,32,1500,1,64]{2,4,3,1,0:T(8,128)(2,1)S(1)}, bf16[2,32,1500,1,64]{2,4,3,1,0:T(8,128)(2,1)}, u32[]{:S(2)}) copy-start(bf16[2,32,1500,1,64]{2,4,3,1,0:T(8,128)(2,1)} %param.27) | copy-start | bytes 36864004
